TPU v7x, 32 devices: a whole 2x2x4 slice. The times are simulated.
32 devices in a mesh: rep: 2 (over y), ada: 4 (over z), tp: 4 (over x, core).
Axes of the slice: x: 2, y: 2, z: 4, core: 2. Of those that a mesh axis runs over, the one named last changes fastest.
Arguments:
- hidden: bfloat16 [256, 8192], P(('rep', 'ada')), parts along dimension 0, may hold values from -6 to 6
- input_norm_gain: bfloat16 [8192], replicated, may hold values from 0.5 to 1.5
- request_adapter: int32 [256], P(('rep', 'ada')), parts along dimension 0, may hold values from 0 to 15, as said below
- cache_fill_length: int32 [256], P(('rep', 'ada')), parts along dimension 0, may hold values from 1 to 512, as said below
- query_weight: bfloat16 [8192, 8192], P('ada', 'tp'), may hold values from -0.0625 to 0.0625
- key_weight: bfloat16 [8192, 1024], P('ada', 'tp'), may hold values from -0.0625 to 0.0625
- value_weight: bfloat16 [8192, 1024], P('ada', 'tp'), may hold values from -0.0625 to 0.0625
- output_weight: bfloat16 [8192, 8192], P('tp', 'ada'), may hold values from -0.0625 to 0.0625
- down_weight_all: bfloat16 [8192, 512], P('tp', 'ada'), may hold values from -0.0625 to 0.0625
- query_up_weight: bfloat16 [256, 8192], P('ada', 'tp'), may hold values from -1.5 to 1.5
- value_up_weight: bfloat16 [256, 1024], P('ada', 'tp'), may hold values from -1.5 to 1.5
- rotated_key_cache: bfloat16 [256, 512, 1024], P(('rep', 'ada'), None, 'tp'), parts along dimension 0, may hold values from -768 to 768
- stored_value_cache: bfloat16 [256, 512, 1024], P(('rep', 'ada'), None, 'tp'), parts along dimension 0, may hold values from -6 to 6
Outputs:
- layer_out: bfloat16 [256, 8192], P(('rep', 'tp'), 'ada'), parts along dimension 0
- new_key: bfloat16 [256, 1024], P(('rep', 'ada'), 'tp'), parts along dimension 0
- new_value: bfloat16 [256, 1024], P(('rep', 'ada'), 'tp'), parts along dimension 0
There are 2 independent parts, one for each index of `rep`. A program takes and returns all parts, laid end to end along the dimension named above; an argument that names none is the same for every part. Nothing has to cross between parts.
Inputs may be any that keep to these rules, and one draw needn't show every extreme that they name: `request_adapter`: among the 32 requests of one ada index (aligned blocks), at most 16 name adapters of one group 4 * o to 4 * o + 3; in every draw one group is named by exactly 16 requests of every block. `cache_fill_length`: within each part of rep the 128 lengths sum to 32768, and some request of each part has exactly 512.
All inputs are finite; a program needn't handle non-finite values.
Results may differ from a plain program's by a relative error of at most 0.012.
The roundings to bfloat16 on the way count: a program that leaves them out, or rounds other values in their place, can miss the bound.
Values may be sent and summed in bfloat16 or wider, within the bound.
No kernel may reach another device: no remote copies, remote signals or barrier semaphores. Data moves between devices by JAX's collectives and lax.ppermute only.
A program may use at most 64 MiB of HBM per device.

v0:
```python
import jax
import jax.numpy as jnp
from jax import lax
from jax.sharding import PartitionSpec as P

QUERY_HEAD_COUNT = 64
KEY_VALUE_HEADS = 8
HEAD_WIDTH = 128
ADAPTER_RANK = 16
ADAPTER_SCALE = 2.0
EPSILON = 1e-05
ROPE_BASE = 500000.0


def rotary(vectors, positions):
    count_rows = vectors.shape[0]
    split_heads = vectors.reshape(count_rows, -1, HEAD_WIDTH)
    halfway = HEAD_WIDTH // 2
    frequency = ROPE_BASE ** (-2.0 * jnp.arange(halfway, dtype=jnp.float32) / HEAD_WIDTH)
    angles = positions.astype(jnp.float32)[:, None] * frequency[None, :]
    cosine = jnp.cos(angles)[:, None, :]
    sine_part = jnp.sin(angles)[:, None, :]
    leading = split_heads[..., :halfway]
    trailing = split_heads[..., halfway:]
    turned = jnp.concatenate(
        [leading * cosine - trailing * sine_part, trailing * cosine + leading * sine_part], axis=-1
    )
    return turned.reshape(count_rows, -1)


def on_device(
    hidden,
    input_norm_gain,
    request_adapter,
    cache_fill_length,
    query_weight,
    key_weight,
    value_weight,
    output_weight,
    down_weight_all,
    query_up_weight,
    value_up_weight,
    rotated_key_cache,
    stored_value_cache,
):
    req_local = hidden.shape[0]
    owners = lax.axis_size("ada")
    tp_index = lax.axis_index("tp")
    portion_width = down_weight_all.shape[0]
    grouped_by_holder = down_weight_all.shape[1] // (2 * ADAPTER_RANK)
    capacity = max(2, (2 * req_local + owners - 1) // owners)
    slot_total = owners * capacity
    q_width = query_weight.shape[1]
    kv_width = key_weight.shape[1]
    widened = hidden.astype(jnp.float32)
    inverse = lax.rsqrt(jnp.mean(widened * widened, axis=-1, keepdims=True) + EPSILON)
    normalized_input = (widened * inverse * input_norm_gain.astype(jnp.float32)[None, :]).astype(
        jnp.bfloat16
    )
    normed_cols, hidden_cols = (
        lax.all_to_all(normalized_input, "ada", split_axis=1, concat_axis=0, tiled=True),
        lax.all_to_all(hidden, "ada", split_axis=1, concat_axis=0, tiled=True),
    )
    owner_of = request_adapter // grouped_by_holder
    sub_of = request_adapter % grouped_by_holder
    row_ids = jnp.arange(req_local, dtype=jnp.int32)
    same_owner = owner_of[:, None] == owner_of[None, :]
    earlier = row_ids[:, None] > row_ids[None, :]
    slot_of = jnp.sum(jnp.logical_and(same_owner, earlier), axis=1)
    target = owner_of * capacity + slot_of
    picker = jnp.arange(slot_total, dtype=jnp.int32)[:, None] == target[None, :]
    my_slice = lax.dynamic_slice_in_dim(
        normalized_input, tp_index * portion_width, portion_width, 1
    )
    send_rows = jnp.dot(
        picker.astype(jnp.bfloat16), my_slice, preferred_element_type=jnp.float32
    ).astype(jnp.bfloat16)
    send_rows = send_rows.reshape(owners, capacity, portion_width)
    row_meta = jnp.stack([sub_of, row_ids], axis=1).astype(jnp.float32)
    send_meta = jnp.dot(
        picker.astype(jnp.float32), row_meta, precision=lax.Precision.HIGHEST
    ).astype(jnp.bfloat16)
    send_meta = send_meta.reshape(owners, capacity, 2)
    rows_in = lax.all_to_all(send_rows, "ada", split_axis=0, concat_axis=0, tiled=True)
    meta_in = lax.all_to_all(send_meta, "ada", split_axis=0, concat_axis=0, tiled=True)
    sources = rows_in.shape[0]
    item_count = rows_in.shape[1]
    flattened_rows = rows_in.reshape(sources * item_count, portion_width)
    value_partial = jnp.dot(flattened_rows, down_weight_all, preferred_element_type=jnp.float32)
    down_projected = lax.psum(value_partial, "tp")
    sub_in = meta_in[..., 0].astype(jnp.int32).reshape(-1)
    column_owner = jnp.arange(value_partial.shape[1], dtype=jnp.int32) // (2 * ADAPTER_RANK)
    chosen = jnp.where(column_owner[None, :] == sub_in[:, None], down_projected, 0.0).astype(
        jnp.bfloat16
    )
    split_rank = chosen.reshape(-1, grouped_by_holder, 2 * ADAPTER_RANK)
    query_down_part = split_rank[:, :, :ADAPTER_RANK].reshape(-1, grouped_by_holder * ADAPTER_RANK)
    value_down_part = split_rank[:, :, ADAPTER_RANK:].reshape(-1, grouped_by_holder * ADAPTER_RANK)
    adapter_update = ADAPTER_SCALE * jnp.concatenate(
        [
            jnp.dot(query_down_part, query_up_weight, preferred_element_type=jnp.float32),
            jnp.dot(value_down_part, value_up_weight, preferred_element_type=jnp.float32),
        ],
        axis=1,
    )
    row_global = jnp.arange(sources, dtype=jnp.int32)[:, None] * req_local + meta_in[..., 1].astype(
        jnp.int32
    )
    adapter_update, row_global = (adapter_update.reshape(sources, item_count, -1), row_global)
    flat_correction = adapter_update.reshape(-1, adapter_update.shape[2])
    flat_target = row_global.reshape(-1)
    term_rows = jnp.concatenate(
        [
            jnp.dot(normed_cols, query_weight, preferred_element_type=jnp.float32),
            jnp.dot(normed_cols, key_weight, preferred_element_type=jnp.float32),
            jnp.dot(normed_cols, value_weight, preferred_element_type=jnp.float32),
        ],
        axis=1,
    )
    picker_in = (
        jnp.arange(req_local * lax.axis_size("ada"), dtype=jnp.int32)[:, None]
        == flat_target[None, :]
    ).astype(jnp.float32)
    placed_in = jnp.dot(picker_in, flat_correction, precision=lax.Precision.HIGHEST)
    filler = jnp.zeros((req_local * lax.axis_size("ada"), kv_width), jnp.float32)
    summed_qkv = lax.psum_scatter(
        term_rows
        + jnp.concatenate([placed_in[:, :q_width], filler, placed_in[:, q_width:]], axis=1),
        "ada",
        scatter_dimension=0,
        tiled=True,
    )
    query_matrix_rows = summed_qkv[:, :q_width]
    key_rows = summed_qkv[:, q_width : q_width + kv_width]
    value_matrix_rows = summed_qkv[:, q_width + kv_width :]
    rotated_query = rotary(query_matrix_rows, cache_fill_length).astype(jnp.bfloat16)
    new_key = rotary(key_rows, cache_fill_length).astype(jnp.bfloat16)
    new_value = value_matrix_rows.astype(jnp.bfloat16)
    kv_local = kv_width // HEAD_WIDTH
    groups = QUERY_HEAD_COUNT // KEY_VALUE_HEADS
    context_len = rotated_key_cache.shape[1]
    score_scale = HEAD_WIDTH ** (-0.5)
    query_heads = rotated_query.reshape(req_local, kv_local, groups, HEAD_WIDTH)
    key_heads = rotated_key_cache.reshape(req_local, context_len, kv_local, HEAD_WIDTH)
    value_heads = stored_value_cache.reshape(req_local, context_len, kv_local, HEAD_WIDTH)
    scores = (
        jnp.einsum("rkgd,rckd->rkgc", query_heads, key_heads, preferred_element_type=jnp.float32)
        * score_scale
    )
    own_score = (
        jnp.einsum(
            "rkgd,rkd->rkg",
            query_heads,
            new_key.reshape(req_local, kv_local, HEAD_WIDTH),
            preferred_element_type=jnp.float32,
        )
        * score_scale
    )
    in_cache = jnp.arange(context_len, dtype=jnp.int32)[None, :] < cache_fill_length[:, None]
    in_cache = in_cache[:, None, None, :]
    masked = jnp.where(in_cache, scores, -1e30)
    row_max = jnp.maximum(jnp.max(masked, axis=-1), own_score)
    exp_terms = jnp.where(in_cache, jnp.exp(masked - row_max[..., None]), 0.0)
    own_exp = jnp.exp(own_score - row_max)
    denominator = jnp.sum(exp_terms, axis=-1) + own_exp
    weights_low = (exp_terms / denominator[..., None]).astype(jnp.bfloat16)
    own_low = (own_exp / denominator).astype(jnp.bfloat16)
    mixed_heads = jnp.einsum(
        "rkgc,rckd->rkgd", weights_low, value_heads, preferred_element_type=jnp.float32
    )
    mixed_heads = mixed_heads + own_low.astype(jnp.float32)[..., None] * new_value.reshape(
        req_local, kv_local, 1, HEAD_WIDTH
    ).astype(jnp.float32)
    context = mixed_heads.reshape(req_local, -1).astype(jnp.bfloat16)
    partial_out = jnp.dot(
        lax.all_gather(context, "ada", axis=0, tiled=True),
        output_weight,
        preferred_element_type=jnp.float32,
    )
    summed = lax.psum_scatter(partial_out, "tp", scatter_dimension=0, tiled=True)
    share_rows = summed.shape[0]
    residual = lax.dynamic_slice_in_dim(hidden_cols, tp_index * share_rows, share_rows, 0).astype(
        jnp.float32
    )
    layer_out = (residual + summed).astype(jnp.bfloat16)
    return (layer_out, new_key, new_value)


def solution(mesh):
    return jax.shard_map(
        on_device,
        mesh=mesh,
        in_specs=(
            P(("rep", "ada"), None),
            P(),
            P(("rep", "ada")),
            P(("rep", "ada")),
            P("ada", "tp"),
            P("ada", "tp"),
            P("ada", "tp"),
            P("tp", "ada"),
            P("tp", "ada"),
            P("ada", "tp"),
            P("ada", "tp"),
            P(("rep", "ada"), None, "tp"),
            P(("rep", "ada"), None, "tp"),
        ),
        out_specs=(P(("rep", "tp"), "ada"), P(("rep", "ada"), "tp"), P(("rep", "ada"), "tp")),
        check_vma=False,
    )
```

profile of v0, /device:TPU:0, one launch (start us, length us, event | category | flops | bytes accessed | tf_op | source)
XLA Modules:
  0.0 159.5 jit_solution(8979767625529145039)
XLA Ops:
  7.2 0.8 fusion.44
  7.9 0.2 convert_reduce_fusion
  8.1 0.1 convolution_convert_fusion.1
  8.3 0.1 reshape.182
  8.3 0.6 copy.51
  9.0 6.3 %all-to-all-start.2 = ((bf16[4,16,2]{1,2,0:T(2,128)(2,1)}), bf16[4,16,2]{1,2,0:T(2,128)(2,1)S(1)}, u32[]{:S(2)}, u32[]{:S(2)}) async-start(bf16[4,16,2]{1,2,0:T(2,128)(2,1)} %copy.51), calls=%async_computation.2 | async-start | bytes 4096 | tf_op jit(solution)/shard_map/all_to_all | solution.py:85
  15.3 0.7 convert_element_type.98
  16.0 1.2 fusion.18
  17.3 1.2 fusion.20
  18.5 0.9 convolution_convert_fusion
  19.4 1.4 all-to-all-done.2
  20.8 3.7 %all-to-all-start.3 = ((bf16[4,16,2048]{2,1,0:T(8,128)(2,1)}), bf16[4,16,2048]{2,1,0:T(8,128)(2,1)S(1)}, u32[]{:S(2)}, u32[]{:S(2)}) async-start(bf16[4,16,2048]{2,1,0:T(8,128)(2,1)} %bitcast.6), calls=%async_computation.3 | async-start | bytes 524288 | tf_op jit(solution)/shard_map/all_to_all | solution.py:84
  24.7 0.8 copy.93
  25.7 7.1 %all-to-all-done.3 = bf16[4,16,2048]{2,1,0:T(8,128)(2,1)S(1)} async-done(((bf16[4,16,2048]{2,1,0:T(8,128)(2,1)}), bf16[4,16,2048]{2,1,0:T(8,128)(2,1)S(1)}, u32[]{:S(2)}, u32[]{:S(2)}) %all-to-all-start.3) | async-done | bytes 262176 | tf_op jit(solution)/shard_map/all_to_all | solution.py:84
  32.9 3.5 %all-to-all-start.1 = ((bf16[32,4,2048]{2,0,1:T(8,128)(2,1)}), bf16[32,4,2048]{2,0,1:T(8,128)(2,1)S(1)}, u32[]{:S(2)}, u32[]{:S(2)}) async-start(bf16[32,4,2048]{2,0,1:T(8,128)(2,1)} %bitcast.93), calls=%async_computation.1 | async-start | bytes 1048576 | tf_op jit(solution)/shard_map/all_to_all | solution.py:61
  36.4 1.3 fusion.57
  37.6 10.6 %psum.7 = bf16[64,128]{1,0:T(8,128)(2,1)S(1)} all-reduce(f32[64,128]{1,0:T(8,128)S(1)} %fusion.57), channel_id=1, replica_groups=mesh['rep'=2,'ada'=4,'tp'=4] {'tp'}, use_global_device_ids=true, to_apply=%region_2.3 | all-reduce | flops 8192 | bytes 49152 | tf_op jit(solution)/shard_map/psum | solution.py:90
  48.3 0.1 copy.52
  48.4 0.9 fusion.59
  49.4 1.2 fusion.58
  50.6 0.6 fusion.22
  51.2 0.1 slice.57
  51.4 4.7 %fusion.54 = f32[128,2048]{1,0:T(8,128)S(1)} fusion(bf16[128,2048]{1,0:T(8,128)(2,1)S(1)} %bitcast.97, bf16[2048,2048]{1,0:T(8,128)(2,1)} %param.17), kind=kOutput, calls=%fused_computation.94 | convolution fusion | flops 1073741824 | bytes 9961472 | tf_op jit(solution)/shard_map/dot_general | solution.py:114
  56.1 0.3 fusion.55
  56.4 0.3 fusion.56
  56.8 1.3 maximum_add_fusion
  58.2 0.1 multiply_cosine_fusion
  58.4 32.9 %reduce-scatter.3.cloned.1.call-done = f32[32,2560]{1,0:T(8,128)} async-done(((f32[128,2560]{1,0:T(8,128)}), f32[32,2560]{1,0:T(8,128)}) %reduce-scatter.3.cloned.1.call-update) | async-done | bytes 327696 | tf_op jit(solution)/shard_map/reduce_scatter | solution.py:126
  91.3 0.8 slice.62
  92.0 1.0 slice_bitcast_fusion
  93.1 0.1 multiply_subtract_fusion
  93.2 0.2 subtract_convert_fusion
  93.4 0.1 fusion.75
  93.5 0.3 fusion.32
  93.8 5.8 %fusion.53 = (f32[32,2,8]{2,1,0:T(2,128)S(1)}, f32[32,2,8,512]{3,2,1,0:T(8,128)S(1)}) fusion(bf16[32,16,64]{2,1,0:T(8,128)(2,1)S(1)} %get-tuple-element.6, bf16[32,16,64]{2,1,0:T(8,128)(2,1)S(1)} %get-tuple-element.5, pred[32,512]{1,0:T(8,128)(4,1)S(1)} %iota_compare_fusion.1, bf16[32,512,256]{2,1,0:T(8,128)(2,1)} %param.24), kind=kOutput, calls=%fused_computation.93 | convolution fusion | flops 68156928 | bytes 9586688 | tf_op jit(solution)/shard_map/rkgd,rckd->rkgc/dot_general | solution.py:147
  99.7 0.1 copy.55
  99.8 0.4 fusion.21
  100.5 0.8 slice.82
  101.3 4.7 %fusion.15 = bf16[32,2,8,128]{3,2,1,0:T(8,128)(2,1)S(1)} fusion(f32[32,2,8,512]{3,2,1,0:T(8,128)S(1)} %get-tuple-element.18, f32[32,2,8]{2,1,0:T(2,128)S(1)} %copy.57, f32[32,2,8]{2,1,0:T(2,128)S(1)} %copy.55, pred[32,512]{1,0:T(8,128)(4,1)S(1)} %iota_compare_fusion.1, f32[32,2,128]{2,1,0:T(2,128)S(1)} %reshape.194, f32[32,2,8]{2,1,0:T(2,128)S(1)} %copy.59, ...), kind=kOutput, calls=%fused_computation.13 | convolution fusion | flops 68354048 | bytes 9623552 | tf_op jit(solution)/shard_map/rkgc,rckd->rkgd/dot_general | solution.py:168
  106.0 16.0 %all_gather.3 = bf16[128,2048]{1,0:T(8,128)(2,1)S(1)} all-gather(bf16[32,2048]{1,0:T(8,128)(2,1)S(1)} %bitcast.105), channel_id=1, replica_groups=mesh['rep'=2,'ada'=4,'tp'=4] {'ada'}, dimensions={0}, use_global_device_ids=true | all-gather | bytes 655360 | tf_op jit(solution)/shard_map/all_gather | solution.py:176
  122.0 5.7 %fusion.60 = f32[128,2048]{1,0:T(8,128)} fusion(bf16[128,2048]{1,0:T(8,128)(2,1)S(1)} %all_gather.3, bf16[2048,2048]{1,0:T(8,128)(2,1)} %param.20), kind=kOutput, calls=%fused_computation.100 | convolution fusion | flops 1073741824 | bytes 9961472 | tf_op jit(solution)/shard_map/dot_general | solution.py:175
  127.7 0.9 copy.94
  128.6 3.5 %all-to-all-start = ((bf16[32,4,2048]{2,0,1:T(8,128)(2,1)}), bf16[32,4,2048]{2,0,1:T(8,128)(2,1)S(1)}, u32[]{:S(2)}, u32[]{:S(2)}) async-start(bf16[32,4,2048]{2,0,1:T(8,128)(2,1)} %bitcast.94), calls=%async_computation | async-start | bytes 1048576 | tf_op jit(solution)/shard_map/all_to_all | solution.py:62
  132.1 0.1 maximum_convert_fusion
  132.2 0.6 copy.96
  132.8 10.1 %all-to-all-done = bf16[32,4,2048]{2,0,1:T(8,128)(2,1)S(1)} async-done(((bf16[32,4,2048]{2,0,1:T(8,128)(2,1)}), bf16[32,4,2048]{2,0,1:T(8,128)(2,1)S(1)}, u32[]{:S(2)}, u32[]{:S(2)}) %all-to-all-start) | async-done | bytes 524320 | tf_op jit(solution)/shard_map/all_to_all | solution.py:62
  142.9 8.1 %reduce-scatter.5.cloned.1.call-done = f32[32,2048]{1,0:T(8,128)} async-done(((f32[128,2048]{1,0:T(8,128)}), f32[32,2048]{1,0:T(8,128)}) %reduce-scatter.5.cloned.1.call-update) | async-done | bytes 262160 | tf_op jit(solution)/shard_map/reduce_scatter | solution.py:180
  151.0 1.6 %add_convert_fusion = bf16[32,2048]{1,0:T(8,128)(2,1)} fusion(f32[32,2048]{1,0:T(8,128)} %reduce-scatter.5.cloned.1.call-done, bf16[128,2048]{1,0:T(8,128)(2,1)S(1)} %bitcast.104, s32[]{:T(128)S(6)} %select_n.38), kind=kLoop, calls=%fused_computation.33 | loop fusion | flops 196608 | bytes 524292 | tf_op jit(solution)/shard_map/convert_element_type | solution.py:185
  (45 shorter events, 1.3 us)
Async XLA Ops:
  7.2 48.9 %copy-start = (bf16[2048,256]{1,0:T(8,128)(2,1)S(1)}, bf16[2048,256]{1,0:T(8,128)(2,1)}, u32[]{:S(2)}) copy-start(bf16[2048,256]{1,0:T(8,128)(2,1)} %param.18) | copy-start | bytes 3145732
  9.0 11.8 %all-to-all-start.2 = ((bf16[4,16,2]{1,2,0:T(2,128)(2,1)}), bf16[4,16,2]{1,2,0:T(2,128)(2,1)S(1)}, u32[]{:S(2)}, u32[]{:S(2)}) async-start(bf16[4,16,2]{1,2,0:T(2,128)(2,1)} %copy.51), calls=%async_computation.2 | async-start | bytes 4096 | tf_op jit(solution)/shard_map/all_to_all | solution.py:85
  20.8 12.0 %all-to-all-start.3 = ((bf16[4,16,2048]{2,1,0:T(8,128)(2,1)}), bf16[4,16,2048]{2,1,0:T(8,128)(2,1)S(1)}, u32[]{:S(2)}, u32[]{:S(2)}) async-start(bf16[4,16,2048]{2,1,0:T(8,128)(2,1)} %bitcast.6), calls=%async_computation.3 | async-start | bytes 524288 | tf_op jit(solution)/shard_map/all_to_all | solution.py:84
  32.9 18.5 %all-to-all-start.1 = ((bf16[32,4,2048]{2,0,1:T(8,128)(2,1)}), bf16[32,4,2048]{2,0,1:T(8,128)(2,1)S(1)}, u32[]{:S(2)}, u32[]{:S(2)}) async-start(bf16[32,4,2048]{2,0,1:T(8,128)(2,1)} %bitcast.93), calls=%async_computation.1 | async-start | bytes 1048576 | tf_op jit(solution)/shard_map/all_to_all | solution.py:61
  36.3 54.9 %reduce-scatter.3.cloned.1.call-start = ((), (), s32[]{:S(2)}) async-start(), calls=%async_computation.6 | async-start | bytes 1638400 | tf_op jit(solution)/shard_map/reduce_scatter | solution.py:126
  51.3 5.1 %copy-start.2 = (bf16[2048,256]{1,0:T(8,128)(2,1)S(1)}, bf16[2048,256]{1,0:T(8,128)(2,1)}, u32[]{:S(2)}) copy-start(bf16[2048,256]{1,0:T(8,128)(2,1)} %param.19) | copy-start | bytes 3145732
  51.3 6.8 %copy-start.4 = (s32[32]{0:T(128)S(1)}, s32[32]{0:T(128)}, u32[]{:S(2)}) copy-start(s32[32]{0:T(128)} %param.16) | copy-start | bytes 388
  58.1 93.0 %reduce-scatter.5.cloned.1.call-start = ((), (), s32[]{:S(2)}) async-start(), calls=%async_computation.7 | async-start | bytes 1310720 | tf_op jit(solution)/shard_map/reduce_scatter | solution.py:180
  101.2 26.4 %copy-start.3 = (bf16[32,256]{1,0:T(8,128)(2,1)}, bf16[32,256]{1,0:T(8,128)(2,1)S(1)}, u32[]{:S(2)}) copy-start(bf16[32,256]{1,0:T(8,128)(2,1)S(1)} %slice.82) | copy-start | bytes 49156
  122.0 5.8 %copy-start.1 = (bf16[32,8192]{1,0:T(8,128)(2,1)S(1)}, bf16[32,8192]{1,0:T(8,128)(2,1)}, u32[]{:S(2)}) copy-start(bf16[32,8192]{1,0:T(8,128)(2,1)} %param.13) | copy-start | bytes 1572868
  128.6 14.3 %all-to-all-start = ((bf16[32,4,2048]{2,0,1:T(8,128)(2,1)}), bf16[32,4,2048]{2,0,1:T(8,128)(2,1)S(1)}, u32[]{:S(2)}, u32[]{:S(2)}) async-start(bf16[32,4,2048]{2,0,1:T(8,128)(2,1)} %bitcast.94), calls=%async_computation | async-start | bytes 1048576 | tf_op jit(solution)/shard_map/all_to_all | solution.py:62
Sparse Core Ops, SparseCore 0:
  58.2 33.0 reduce-scatter.2
  127.8 23.1 reduce-scatter.4
where the time goes:
time: 160 us; the launch traced here: 159 us
  waiting for transfers between devices  59.6 us (37%)
  matrix products  26.9 us (17%)
  blocking collectives  26.5 us (17%)
  starting transfers between devices  17.1 us (11%)
  between operations  14.3 us (9%)
  other arithmetic  8.31 us (5%)
  local copies, waits for them, and re-layouts  6.7 us (4%)
    reduce_scatter x1, waiting for transfers between devices, on_device(): lax.psum_scatter(term_rows + jnp.concatenate([placed_in[:, :q_width], fil...  32.9 us
    all_gather x1, blocking collectives, on_device(): lax.all_gather(context, 'ada', axis=0, tiled=True)  16 us
    psum x1, blocking collectives, on_device(): down_projected = lax.psum(value_partial, 'tp')  10.6 us
    all_to_all x1, waiting for transfers between devices, on_device(): lax.all_to_all(hidden, 'ada', split_axis=1, concat_axis=0, tiled=True)  10.1 us
    reduce_scatter x1, waiting for transfers between devices, on_device(): lax.psum_scatter(partial_out, 'tp', scatter_dimension=0, tiled=True)  8.12 us
    all_to_all x1, waiting for transfers between devices, on_device(): lax.all_to_all(send_rows, 'ada', split_axis=0, concat_axis=0, tiled=True)  7.11 us
    all_to_all x1, starting transfers between devices, on_device(): lax.all_to_all(send_meta, 'ada', split_axis=0, concat_axis=0, tiled=True)  6.35 us
    dot_general x1, matrix products, on_device(): jnp.einsum('rkgd,rckd->rkgc', query_heads, key_heads, preferred_element_t...  5.81 us
  transfers between devices with their start and end apart: 6, of which 5 were waited for; matrix products, arithmetic and copies ran while one was open for 7% of the time, Pallas kernels for 0%

commit v1 on v0

--- a/solution.py
+++ b/solution.py
@@ -87,7 +87,11 @@
     item_count = rows_in.shape[1]
     flattened_rows = rows_in.reshape(sources * item_count, portion_width)
     value_partial = jnp.dot(flattened_rows, down_weight_all, preferred_element_type=jnp.float32)
-    down_projected = lax.psum(value_partial, "tp")
+    down_projected = value_partial
+    for hop in (1, 2):
+        down_projected = down_projected + lax.ppermute(
+            down_projected, "tp", [(dev, dev ^ hop) for dev in range(4)]
+        )
     sub_in = meta_in[..., 0].astype(jnp.int32).reshape(-1)
     column_owner = jnp.arange(value_partial.shape[1], dtype=jnp.int32) // (2 * ADAPTER_RANK)
     chosen = jnp.where(column_owner[None, :] == sub_in[:, None], down_projected, 0.0).astype(

time: 160 us -> 160 us (level)
  blocking collectives: 26.5 us -> 15.9 us
  waiting for transfers between devices: 59.6 us -> 68.8 us
    all_to_all x1, waiting for transfers between devices: 0.01 us -> 11.4 us  [on_device(): lax.all_to_all(normalized_input, 'ada', split_axis=1, concat_axis=0, tile...]
    psum x1 -> x0, blocking collectives: 10.6 us -> none  [on_device(): down_projected = lax.psum(value_partial, 'tp')]
    reduce_scatter x1, waiting for transfers between devices: 32.9 us -> 29.4 us  [on_device(): lax.psum_scatter(term_rows + jnp.concatenate([placed_in[:, :q_width], fil...]
    all_to_all x1, starting transfers between devices: 6.35 us -> 3.22 us  [on_device(): lax.all_to_all(send_meta, 'ada', split_axis=0, concat_axis=0, tiled=True)]
    all_to_all x1, starting transfers between devices: 3.74 us -> 6.35 us  [on_device(): lax.all_to_all(send_rows, 'ada', split_axis=0, concat_axis=0, tiled=True)]
  transfers between devices with their start and end apart: 6 -> 8, of which waited for: 5 -> 7; matrix products, arithmetic and copies ran while one was open for 7% -> 5% of each run, Pallas kernels for 0% -> 0%
where the time goes in v1:
time: 160 us; the launch traced here: 159 us
  waiting for transfers between devices  68.8 us (43%)
  matrix products  26.9 us (17%)
  starting transfers between devices  18.3 us (11%)
  blocking collectives  15.9 us (10%)
  between operations  14.3 us (9%)
  other arithmetic  8.31 us (5%)
  local copies, waits for them, and re-layouts  6.69 us (4%)
    reduce_scatter x1, waiting for transfers between devices, on_device(): lax.psum_scatter(term_rows + jnp.concatenate([placed_in[:, :q_width], fil...  29.4 us
    all_gather x1, blocking collectives, on_device(): lax.all_gather(context, 'ada', axis=0, tiled=True)  15.9 us
    all_to_all x1, waiting for transfers between devices, on_device(): lax.all_to_all(normalized_input, 'ada', split_axis=1, concat_axis=0, tile...  11.4 us
    all_to_all x1, waiting for transfers between devices, on_device(): lax.all_to_all(hidden, 'ada', split_axis=1, concat_axis=0, tiled=True)  10.1 us
    reduce_scatter x1, waiting for transfers between devices, on_device(): lax.psum_scatter(partial_out, 'tp', scatter_dimension=0, tiled=True)  8.09 us
    all_to_all x1, waiting for transfers between devices, on_device(): lax.all_to_all(send_rows, 'ada', split_axis=0, concat_axis=0, tiled=True)  8.07 us
    all_to_all x1, starting transfers between devices, on_device(): lax.all_to_all(send_rows, 'ada', split_axis=0, concat_axis=0, tiled=True)  6.35 us
    dot_general x1, matrix products, on_device(): jnp.einsum('rkgd,rckd->rkgc', query_heads, key_heads, preferred_element_t...  5.81 us
  transfers between devices with their start and end apart: 8, of which 7 were waited for; matrix products, arithmetic and copies ran while one was open for 5% of the time, Pallas kernels for 0%

profile of v1, /device:TPU:0, one launch (start us, length us, event | category | flops | bytes accessed | tf_op | source)
XLA Modules:
  0.0 159.1 jit_solution(14084791862385536307)
XLA Ops:
  7.2 0.8 fusion.44
  7.9 0.2 convert_reduce_fusion
  8.1 0.7 convert_element_type.98
  8.9 1.2 fusion.18
  10.1 1.2 fusion.20
  11.4 0.9 convolution_convert_fusion
  12.3 6.3 %all-to-all-start.3 = ((bf16[4,16,2048]{2,1,0:T(8,128)(2,1)}), bf16[4,16,2048]{2,1,0:T(8,128)(2,1)S(1)}, u32[]{:S(2)}, u32[]{:S(2)}) async-start(bf16[4,16,2048]{2,1,0:T(8,128)(2,1)} %bitcast.6), calls=%async_computation.3 | async-start | bytes 524288 | tf_op jit(solution)/shard_map/all_to_all | solution.py:84
  18.6 0.1 convolution_convert_fusion.1
  18.8 0.6 copy.51
  19.5 8.1 %all-to-all-done.3 = bf16[4,16,2048]{2,1,0:T(8,128)(2,1)S(1)} async-done(((bf16[4,16,2048]{2,1,0:T(8,128)(2,1)}), bf16[4,16,2048]{2,1,0:T(8,128)(2,1)S(1)}, u32[]{:S(2)}, u32[]{:S(2)}) %all-to-all-start.3) | async-done | bytes 262176 | tf_op jit(solution)/shard_map/all_to_all | solution.py:84
  27.5 3.2 %all-to-all-start.2 = ((bf16[4,16,2]{1,2,0:T(2,128)(2,1)}), bf16[4,16,2]{1,2,0:T(2,128)(2,1)S(1)}, u32[]{:S(2)}, u32[]{:S(2)}) async-start(bf16[4,16,2]{1,2,0:T(2,128)(2,1)} %copy.51), calls=%async_computation.2 | async-start | bytes 4096 | tf_op jit(solution)/shard_map/all_to_all | solution.py:85
  30.8 1.3 fusion.57
  32.3 0.8 copy.93
  33.1 0.2 collective-permute-done
  33.3 1.5 collective-permute-start.1
  34.8 1.4 all-to-all-done.2
  36.2 3.6 %all-to-all-start.1 = ((bf16[32,4,2048]{2,0,1:T(8,128)(2,1)}), bf16[32,4,2048]{2,0,1:T(8,128)(2,1)S(1)}, u32[]{:S(2)}, u32[]{:S(2)}) async-start(bf16[32,4,2048]{2,0,1:T(8,128)(2,1)} %bitcast.93), calls=%async_computation.1 | async-start | bytes 1048576 | tf_op jit(solution)/shard_map/all_to_all | solution.py:61
  40.1 0.1 copy.52
  40.3 0.9 fusion.59
  41.2 1.2 fusion.58
  42.4 0.6 fusion.22
  43.0 0.1 slice.57
  43.2 11.4 %all-to-all-done.1 = bf16[32,4,2048]{2,0,1:T(8,128)(2,1)S(1)} async-done(((bf16[32,4,2048]{2,0,1:T(8,128)(2,1)}), bf16[32,4,2048]{2,0,1:T(8,128)(2,1)S(1)}, u32[]{:S(2)}, u32[]{:S(2)}) %all-to-all-start.1) | async-done | bytes 524320 | tf_op jit(solution)/shard_map/all_to_all | solution.py:61
  54.6 4.7 %fusion.54 = f32[128,2048]{1,0:T(8,128)S(1)} fusion(bf16[128,2048]{1,0:T(8,128)(2,1)S(1)} %bitcast.97, bf16[2048,2048]{1,0:T(8,128)(2,1)} %param.17), kind=kOutput, calls=%fused_computation.94 | convolution fusion | flops 1073741824 | bytes 9961472 | tf_op jit(solution)/shard_map/dot_general | solution.py:118
  59.3 0.3 fusion.55
  59.7 0.3 fusion.56
  60.0 1.3 maximum_add_fusion
  61.5 0.1 multiply_cosine_fusion
  61.6 29.4 %reduce-scatter.3.cloned.1.call-done = f32[32,2560]{1,0:T(8,128)} async-done(((f32[128,2560]{1,0:T(8,128)}), f32[32,2560]{1,0:T(8,128)}) %reduce-scatter.3.cloned.1.call-update) | async-done | bytes 327696 | tf_op jit(solution)/shard_map/reduce_scatter | solution.py:130
  91.0 0.8 slice.62
  91.8 1.0 slice_bitcast_fusion
  92.8 0.1 multiply_subtract_fusion
  92.9 0.2 subtract_convert_fusion
  93.1 0.1 fusion.75
  93.2 0.3 fusion.32
  93.6 5.8 %fusion.53 = (f32[32,2,8]{2,1,0:T(2,128)S(1)}, f32[32,2,8,512]{3,2,1,0:T(8,128)S(1)}) fusion(bf16[32,16,64]{2,1,0:T(8,128)(2,1)S(1)} %get-tuple-element.6, bf16[32,16,64]{2,1,0:T(8,128)(2,1)S(1)} %get-tuple-element.5, pred[32,512]{1,0:T(8,128)(4,1)S(1)} %iota_compare_fusion.1, bf16[32,512,256]{2,1,0:T(8,128)(2,1)} %param.24), kind=kOutput, calls=%fused_computation.93 | convolution fusion | flops 68156928 | bytes 9586688 | tf_op jit(solution)/shard_map/rkgd,rckd->rkgc/dot_general | solution.py:151
  99.5 0.4 fusion.21
  100.2 0.8 slice.82
  101.0 4.7 %fusion.15 = bf16[32,2,8,128]{3,2,1,0:T(8,128)(2,1)S(1)} fusion(f32[32,2,8,512]{3,2,1,0:T(8,128)S(1)} %get-tuple-element.18, f32[32,2,8]{2,1,0:T(2,128)S(1)} %copy.57, f32[32,2,8]{2,1,0:T(2,128)S(1)} %copy.55, pred[32,512]{1,0:T(8,128)(4,1)S(1)} %iota_compare_fusion.1, f32[32,2,128]{2,1,0:T(2,128)S(1)} %reshape.194, f32[32,2,8]{2,1,0:T(2,128)S(1)} %copy.59, ...), kind=kOutput, calls=%fused_computation.13 | convolution fusion | flops 68354048 | bytes 9623552 | tf_op jit(solution)/shard_map/rkgc,rckd->rkgd/dot_general | solution.py:172
  105.8 15.9 %all_gather.3 = bf16[128,2048]{1,0:T(8,128)(2,1)S(1)} all-gather(bf16[32,2048]{1,0:T(8,128)(2,1)S(1)} %bitcast.105), channel_id=1, replica_groups=mesh['rep'=2,'ada'=4,'tp'=4] {'ada'}, dimensions={0}, use_global_device_ids=true | all-gather | bytes 655360 | tf_op jit(solution)/shard_map/all_gather | solution.py:180
  121.7 5.7 %fusion.60 = f32[128,2048]{1,0:T(8,128)} fusion(bf16[128,2048]{1,0:T(8,128)(2,1)S(1)} %all_gather.3, bf16[2048,2048]{1,0:T(8,128)(2,1)} %param.20), kind=kOutput, calls=%fused_computation.100 | convolution fusion | flops 1073741824 | bytes 9961472 | tf_op jit(solution)/shard_map/dot_general | solution.py:179
  127.4 0.8 copy.94
  128.3 3.5 %all-to-all-start = ((bf16[32,4,2048]{2,0,1:T(8,128)(2,1)}), bf16[32,4,2048]{2,0,1:T(8,128)(2,1)S(1)}, u32[]{:S(2)}, u32[]{:S(2)}) async-start(bf16[32,4,2048]{2,0,1:T(8,128)(2,1)} %bitcast.94), calls=%async_computation | async-start | bytes 1048576 | tf_op jit(solution)/shard_map/all_to_all | solution.py:62
  131.7 0.1 maximum_convert_fusion
  131.8 0.6 copy.96
  132.5 10.1 %all-to-all-done = bf16[32,4,2048]{2,0,1:T(8,128)(2,1)S(1)} async-done(((bf16[32,4,2048]{2,0,1:T(8,128)(2,1)}), bf16[32,4,2048]{2,0,1:T(8,128)(2,1)S(1)}, u32[]{:S(2)}, u32[]{:S(2)}) %all-to-all-start) | async-done | bytes 524320 | tf_op jit(solution)/shard_map/all_to_all | solution.py:62
  142.6 8.1 %reduce-scatter.5.cloned.1.call-done = f32[32,2048]{1,0:T(8,128)} async-done(((f32[128,2048]{1,0:T(8,128)}), f32[32,2048]{1,0:T(8,128)}) %reduce-scatter.5.cloned.1.call-update) | async-done | bytes 262160 | tf_op jit(solution)/shard_map/reduce_scatter | solution.py:184
  150.7 1.6 %add_convert_fusion = bf16[32,2048]{1,0:T(8,128)(2,1)} fusion(f32[32,2048]{1,0:T(8,128)} %reduce-scatter.5.cloned.1.call-done, bf16[128,2048]{1,0:T(8,128)(2,1)S(1)} %bitcast.104, s32[]{:T(128)S(6)} %select_n.38), kind=kLoop, calls=%fused_computation.33 | loop fusion | flops 196608 | bytes 524292 | tf_op jit(solution)/shard_map/convert_element_type | solution.py:189
  (49 shorter events, 1.5 us)
Async XLA Ops:
  7.2 52.2 %copy-start = (bf16[2048,256]{1,0:T(8,128)(2,1)S(1)}, bf16[2048,256]{1,0:T(8,128)(2,1)}, u32[]{:S(2)}) copy-start(bf16[2048,256]{1,0:T(8,128)(2,1)} %param.18) | copy-start | bytes 3145732
  12.3 15.3 %all-to-all-start.3 = ((bf16[4,16,2048]{2,1,0:T(8,128)(2,1)}), bf16[4,16,2048]{2,1,0:T(8,128)(2,1)S(1)}, u32[]{:S(2)}, u32[]{:S(2)}) async-start(bf16[4,16,2048]{2,1,0:T(8,128)(2,1)} %bitcast.6), calls=%async_computation.3 | async-start | bytes 524288 | tf_op jit(solution)/shard_map/all_to_all | solution.py:84
  27.5 8.7 %all-to-all-start.2 = ((bf16[4,16,2]{1,2,0:T(2,128)(2,1)}), bf16[4,16,2]{1,2,0:T(2,128)(2,1)S(1)}, u32[]{:S(2)}, u32[]{:S(2)}) async-start(bf16[4,16,2]{1,2,0:T(2,128)(2,1)} %copy.51), calls=%async_computation.2 | async-start | bytes 4096 | tf_op jit(solution)/shard_map/all_to_all | solution.py:85
  32.0 1.3 collective-permute-start
  33.3 6.8 %collective-permute-start.1 = (f32[64,128]{1,0:T(8,128)S(1)}, f32[64,128]{1,0:T(8,128)S(1)}, u32[]{:S(2)}, u32[]{:S(2)}) collective-permute-start(f32[64,128]{1,0:T(8,128)S(1)} %add.83), channel_id=1, source_target_pairs={{0,2},{1,3},{2,0},{3,1},{4,6},{5,7},{6,4},{7,5},{8,10},{9,11},{10,... | collective-permute-start | bytes 98312 | tf_op jit(solution)/shard_map/ppermute | solution.py:92
  36.2 18.4 %all-to-all-start.1 = ((bf16[32,4,2048]{2,0,1:T(8,128)(2,1)}), bf16[32,4,2048]{2,0,1:T(8,128)(2,1)S(1)}, u32[]{:S(2)}, u32[]{:S(2)}) async-start(bf16[32,4,2048]{2,0,1:T(8,128)(2,1)} %bitcast.93), calls=%async_computation.1 | async-start | bytes 1048576 | tf_op jit(solution)/shard_map/all_to_all | solution.py:61
  39.9 51.1 %reduce-scatter.3.cloned.1.call-start = ((), (), s32[]{:S(2)}) async-start(), calls=%async_computation.6 | async-start | bytes 1638400 | tf_op jit(solution)/shard_map/reduce_scatter | solution.py:130
  54.6 5.1 %copy-start.2 = (bf16[2048,256]{1,0:T(8,128)(2,1)S(1)}, bf16[2048,256]{1,0:T(8,128)(2,1)}, u32[]{:S(2)}) copy-start(bf16[2048,256]{1,0:T(8,128)(2,1)} %param.19) | copy-start | bytes 3145732
  54.6 6.7 %copy-start.4 = (s32[32]{0:T(128)S(1)}, s32[32]{0:T(128)}, u32[]{:S(2)}) copy-start(s32[32]{0:T(128)} %param.16) | copy-start | bytes 388
  61.3 89.4 %reduce-scatter.5.cloned.1.call-start = ((), (), s32[]{:S(2)}) async-start(), calls=%async_computation.7 | async-start | bytes 1310720 | tf_op jit(solution)/shard_map/reduce_scatter | solution.py:184
  101.0 26.4 %copy-start.3 = (bf16[32,256]{1,0:T(8,128)(2,1)}, bf16[32,256]{1,0:T(8,128)(2,1)S(1)}, u32[]{:S(2)}) copy-start(bf16[32,256]{1,0:T(8,128)(2,1)S(1)} %slice.82) | copy-start | bytes 49156
  121.7 5.7 %copy-start.1 = (bf16[32,8192]{1,0:T(8,128)(2,1)S(1)}, bf16[32,8192]{1,0:T(8,128)(2,1)}, u32[]{:S(2)}) copy-start(bf16[32,8192]{1,0:T(8,128)(2,1)} %param.13) | copy-start | bytes 1572868
  128.3 14.3 %all-to-all-start = ((bf16[32,4,2048]{2,0,1:T(8,128)(2,1)}), bf16[32,4,2048]{2,0,1:T(8,128)(2,1)S(1)}, u32[]{:S(2)}, u32[]{:S(2)}) async-start(bf16[32,4,2048]{2,0,1:T(8,128)(2,1)} %bitcast.94), calls=%async_computation | async-start | bytes 1048576 | tf_op jit(solution)/shard_map/all_to_all | solution.py:62
Sparse Core Ops, SparseCore 0:
  61.4 29.5 reduce-scatter.2
  127.5 23.0 reduce-scatter.4
